TPU v7x, 128 devices: a whole 4x4x4 slice. The times are simulated.
128 devices in a mesh: pair: 32 (over y, z, x_hi), aux: 4 (over x_lo, core).
Axes of the slice: x: 4 (x_hi: 2, x_lo: 2; x = x_hi * 2 + x_lo), y: 4, z: 4, core: 2. Of those that a mesh axis runs over, the one named last changes fastest.
Arguments:
- pair_factors: bfloat16 [65536, 16384], P('pair', 'aux'), may hold values from -0.048913987 to 0.048913987
- pair_weights: float32 [65536], P('pair'), may hold values from 0.08 to 0.8
- probes: float32 [16384, 64], P('aux'), may hold values from -12 to 12
Outputs:
- last_vectors: float32 [16384, 64], P('aux', 'pair')
- moments: float32 [9], replicated
- energy: float32 [1], replicated
All inputs are finite; a program needn't handle non-finite values.
Results may differ from a plain program's by a relative error of at most 0.019.
Values may be sent and summed in bfloat16 or wider, within the bound.
A program may use at most 64 MiB of HBM per device.

v0:
```python
import functools

import jax
import jax.numpy as jnp
import numpy as np
from jax import lax
from jax.sharding import Mesh
from jax.sharding import PartitionSpec as P

ITERS = 8
AUX = ("aux_0", "aux_1")
PAIR = ("pair_0", "pair_1", "pair_2")
PAIR_AUX = ("pair_0", "pair_1", "pair_2", "aux_0", "aux_1")


spread = 5.0


def sent_to_all(shard, axis):
    copies = jnp.broadcast_to(shard, (lax.axis_size(axis), *shard.shape))
    return lax.all_to_all(copies, axis, split_axis=0, concat_axis=0, tiled=True)


def of_everyone(shard, axis):
    return sent_to_all(shard, axis).sum(axis=0)


def in_blocks(shard, dim, size):
    lengths = shard.shape
    blocks = shard.reshape(*lengths[:dim], size, lengths[dim] // size, *lengths[dim + 1 :])
    return jnp.moveaxis(blocks, dim, 0)


def summed_on_arrival(shard, axis, dim):
    blocks = in_blocks(shard, dim, lax.axis_size(axis))
    arrived = lax.all_to_all(blocks, axis, split_axis=0, concat_axis=0, tiled=True)
    return arrived.sum(axis=0)


def joined_along(blocks, dim):
    blocks = jnp.moveaxis(blocks, 0, dim)
    lengths = blocks.shape
    return blocks.reshape(*lengths[:dim], lengths[dim] * lengths[dim + 1], *lengths[dim + 2 :])


def gather_directly(shard, axis, dim):
    return joined_along(sent_to_all(shard, axis), dim)


def by_axis(shard, axes):
    return functools.reduce(lax.psum, axes, shard)


def cheb_coefficients(order_count):
    node_count = 64
    angles = (np.arange(node_count) + 0.5) * np.pi / node_count
    samples = np.log(1.0 + spread * (np.cos(angles) + 1.0) / 2.0)
    values = [
        2.0 / node_count * np.sum(samples * np.cos(degree * angles))
        for degree in range(order_count)
    ]
    values[0] = values[0] / 2.0
    return np.array(values)


def per_device(pair_factors, pair_weights, probes):
    probe_total = probes.shape[1]
    divisor = probe_total * probes.shape[0] * lax.axis_size(AUX)
    share = probe_total // lax.axis_size(PAIR)
    start = lax.axis_index(PAIR) * share
    own_probes = lax.dynamic_slice_in_dim(probes, start, share, 1)
    partials = [jnp.sum(own_probes * own_probes)]
    previous = own_probes
    own_share = own_probes
    gathered = probes.astype(jnp.bfloat16)
    for degree in range(ITERS):
        rows = jnp.dot(pair_factors, gathered, preferred_element_type=jnp.float32)
        rows = of_everyone(rows, AUX)
        scaled = (pair_weights[:, None] * rows).astype(jnp.bfloat16)
        image = summed_on_arrival(
            lax.dot_general(
                pair_factors, scaled, (((0,), (0,)), ((), ())), preferred_element_type=jnp.float32
            ),
            PAIR,
            1,
        )
        mapped = 2.0 / spread * image - own_share
        following = mapped if degree == 0 else 2.0 * mapped - previous
        previous, own_share = (own_share, following)
        partials.append(jnp.sum(own_probes * own_share))
        if degree + 1 < ITERS:
            gathered = gather_directly(own_share.astype(jnp.bfloat16), PAIR, 1)
    totals = by_axis(jnp.stack(partials), PAIR_AUX)
    moments = totals / divisor
    coefficients = jnp.asarray(cheb_coefficients(ITERS + 1)).astype(moments.dtype)
    energy = jnp.sum(coefficients * moments).reshape(1)
    return (own_share, moments, energy)


def solution(mesh):
    torus = Mesh(
        mesh.devices.reshape(4, 4, 2, 2, 2), ("pair_0", "pair_1", "pair_2", "aux_0", "aux_1")
    )
    return jax.shard_map(
        per_device,
        mesh=torus,
        in_specs=(P(PAIR, AUX), P(PAIR), P(AUX, None)),
        out_specs=(P(AUX, PAIR), P(), P()),
        check_vma=False,
    )
```

profile of v0, /device:TPU:1, one launch (start us, length us, event | category | flops | bytes accessed | tf_op | source)
XLA Modules:
  0.0 744.0 jit_solution(20502665536933196)
XLA Ops:
  0.6 11.2 %fusion = f32[2048,64]{0,1:T(8,128)S(1)} fusion(bf16[2048,4096]{1,0:T(8,128)(2,1)} %param.4, f32[4096,64]{0,1:T(8,128)} %param.6), kind=kOutput, calls=%fused_computation.23 | convolution fusion | flops 1074003968 | bytes 18350080 | tf_op jit(solution)/shard_map/dot_general | solution.py:77
  12.1 28.7 %all_to_all.115 = f32[4,2048,64]{1,2,0:T(8,128)S(1)} all-to-all(f32[4,2048,64]{1,2,0:T(8,128)S(1)} %broadcast_in_dim.53), channel_id=1, replica_groups=mesh['pair_0'=4,'pair_1'=4,'pair_2'=2,'aux_0'=2,'aux_1'=2] {'aux_0','aux..., dimensions={0} | all-to-all | bytes 4194304 | tf_op jit(solution)/shard_map/all_to_all | solution.py:21
  61.8 17.8 %all-to-all-done.1 = f32[32,4096,2]{1,2,0:T(2,128)S(1)} async-done(((f32[32,4096,2]{1,2,0:T(2,128)}), f32[32,4096,2]{1,2,0:T(2,128)S(1)}, u32[]{:S(2)}, u32[]{:S(2)}) %all-to-all-start.1) | async-done | bytes 1048608 | tf_op jit(solution)/shard_map/all_to_all | solution.py:36
  81.3 14.9 %all_to_all.116 = bf16[32,4096,2]{1,2,0:T(2,128)(2,1)S(1)} all-to-all(bf16[32,4096,2]{1,2,0:T(2,128)(2,1)S(1)} %broadcast_in_dim.54), channel_id=1, replica_groups=mesh['pair_0'=4,'pair_1'=4,'pair_2'=2,'aux_0'=2,'aux_1'=2] {'pair_0','pa..., dimensions={0} | all-to-all | bytes 1048576 | tf_op jit(solution)/shard_map/all_to_all | solution.py:21
  107.7 30.6 %all_to_all.117 = f32[4,2048,64]{1,2,0:T(8,128)S(1)} all-to-all(f32[4,2048,64]{1,2,0:T(8,128)S(1)} %broadcast_in_dim.55), channel_id=1, replica_groups=mesh['pair_0'=4,'pair_1'=4,'pair_2'=2,'aux_0'=2,'aux_1'=2] {'aux_0','aux..., dimensions={0} | all-to-all | bytes 4194304 | tf_op jit(solution)/shard_map/all_to_all | solution.py:21
  147.9 20.9 %all_to_all.118 = f32[32,4096,2]{1,2,0:T(2,128)S(1)} all-to-all(f32[32,4096,2]{1,2,0:T(2,128)S(1)} %bitcast.108), channel_id=1, replica_groups=mesh['pair_0'=4,'pair_1'=4,'pair_2'=2,'aux_0'=2,'aux_1'=2] {'pair_0','pa..., dimensions={0} | all-to-all | bytes 2097152 | tf_op jit(solution)/shard_map/all_to_all | solution.py:36
  170.5 14.9 %all_to_all.119 = bf16[32,4096,2]{1,2,0:T(2,128)(2,1)S(1)} all-to-all(bf16[32,4096,2]{1,2,0:T(2,128)(2,1)S(1)} %broadcast_in_dim.56), channel_id=1, replica_groups=mesh['pair_0'=4,'pair_1'=4,'pair_2'=2,'aux_0'=2,'aux_1'=2] {'pair_0','pa..., dimensions={0} | all-to-all | bytes 1048576 | tf_op jit(solution)/shard_map/all_to_all | solution.py:21
  196.9 30.6 %all_to_all.120 = f32[4,2048,64]{1,2,0:T(8,128)S(1)} all-to-all(f32[4,2048,64]{1,2,0:T(8,128)S(1)} %broadcast_in_dim.57), channel_id=1, replica_groups=mesh['pair_0'=4,'pair_1'=4,'pair_2'=2,'aux_0'=2,'aux_1'=2] {'aux_0','aux..., dimensions={0} | all-to-all | bytes 4194304 | tf_op jit(solution)/shard_map/all_to_all | solution.py:21
  237.1 20.9 %all_to_all.121 = f32[32,4096,2]{1,2,0:T(2,128)S(1)} all-to-all(f32[32,4096,2]{1,2,0:T(2,128)S(1)} %bitcast.109), channel_id=1, replica_groups=mesh['pair_0'=4,'pair_1'=4,'pair_2'=2,'aux_0'=2,'aux_1'=2] {'pair_0','pa..., dimensions={0} | all-to-all | bytes 2097152 | tf_op jit(solution)/shard_map/all_to_all | solution.py:36
  259.8 15.2 %all_to_all.122 = bf16[32,4096,2]{1,2,0:T(2,128)(2,1)S(1)} all-to-all(bf16[32,4096,2]{1,2,0:T(2,128)(2,1)S(1)} %broadcast_in_dim.58), channel_id=1, replica_groups=mesh['pair_0'=4,'pair_1'=4,'pair_2'=2,'aux_0'=2,'aux_1'=2] {'pair_0','pa..., dimensions={0} | all-to-all | bytes 1048576 | tf_op jit(solution)/shard_map/all_to_all | solution.py:21
  286.4 30.6 %all_to_all.123 = f32[4,2048,64]{1,2,0:T(8,128)S(1)} all-to-all(f32[4,2048,64]{1,2,0:T(8,128)S(1)} %broadcast_in_dim.59), channel_id=1, replica_groups=mesh['pair_0'=4,'pair_1'=4,'pair_2'=2,'aux_0'=2,'aux_1'=2] {'aux_0','aux..., dimensions={0} | all-to-all | bytes 4194304 | tf_op jit(solution)/shard_map/all_to_all | solution.py:21
  326.6 20.9 %all_to_all.124 = f32[32,4096,2]{1,2,0:T(2,128)S(1)} all-to-all(f32[32,4096,2]{1,2,0:T(2,128)S(1)} %bitcast.110), channel_id=1, replica_groups=mesh['pair_0'=4,'pair_1'=4,'pair_2'=2,'aux_0'=2,'aux_1'=2] {'pair_0','pa..., dimensions={0} | all-to-all | bytes 2097152 | tf_op jit(solution)/shard_map/all_to_all | solution.py:36
  348.3 14.9 %all_to_all.125 = bf16[32,4096,2]{1,2,0:T(2,128)(2,1)S(1)} all-to-all(bf16[32,4096,2]{1,2,0:T(2,128)(2,1)S(1)} %broadcast_in_dim.60), channel_id=1, replica_groups=mesh['pair_0'=4,'pair_1'=4,'pair_2'=2,'aux_0'=2,'aux_1'=2] {'pair_0','pa..., dimensions={0} | all-to-all | bytes 1048576 | tf_op jit(solution)/shard_map/all_to_all | solution.py:21
  374.6 30.6 %all_to_all.126 = f32[4,2048,64]{1,2,0:T(8,128)S(1)} all-to-all(f32[4,2048,64]{1,2,0:T(8,128)S(1)} %broadcast_in_dim.61), channel_id=1, replica_groups=mesh['pair_0'=4,'pair_1'=4,'pair_2'=2,'aux_0'=2,'aux_1'=2] {'aux_0','aux..., dimensions={0} | all-to-all | bytes 4194304 | tf_op jit(solution)/shard_map/all_to_all | solution.py:21
  414.8 20.9 %all_to_all.127 = f32[32,4096,2]{1,2,0:T(2,128)S(1)} all-to-all(f32[32,4096,2]{1,2,0:T(2,128)S(1)} %bitcast.111), channel_id=1, replica_groups=mesh['pair_0'=4,'pair_1'=4,'pair_2'=2,'aux_0'=2,'aux_1'=2] {'pair_0','pa..., dimensions={0} | all-to-all | bytes 2097152 | tf_op jit(solution)/shard_map/all_to_all | solution.py:36
  436.6 14.9 %all_to_all.128 = bf16[32,4096,2]{1,2,0:T(2,128)(2,1)S(1)} all-to-all(bf16[32,4096,2]{1,2,0:T(2,128)(2,1)S(1)} %broadcast_in_dim.62), channel_id=1, replica_groups=mesh['pair_0'=4,'pair_1'=4,'pair_2'=2,'aux_0'=2,'aux_1'=2] {'pair_0','pa..., dimensions={0} | all-to-all | bytes 1048576 | tf_op jit(solution)/shard_map/all_to_all | solution.py:21
  462.9 30.6 %all_to_all.129 = f32[4,2048,64]{1,2,0:T(8,128)S(1)} all-to-all(f32[4,2048,64]{1,2,0:T(8,128)S(1)} %broadcast_in_dim.63), channel_id=1, replica_groups=mesh['pair_0'=4,'pair_1'=4,'pair_2'=2,'aux_0'=2,'aux_1'=2] {'aux_0','aux..., dimensions={0} | all-to-all | bytes 4194304 | tf_op jit(solution)/shard_map/all_to_all | solution.py:21
  503.1 20.9 %all_to_all.130 = f32[32,4096,2]{1,2,0:T(2,128)S(1)} all-to-all(f32[32,4096,2]{1,2,0:T(2,128)S(1)} %bitcast.112), channel_id=1, replica_groups=mesh['pair_0'=4,'pair_1'=4,'pair_2'=2,'aux_0'=2,'aux_1'=2] {'pair_0','pa..., dimensions={0} | all-to-all | bytes 2097152 | tf_op jit(solution)/shard_map/all_to_all | solution.py:36
  524.9 14.9 %all_to_all.131 = bf16[32,4096,2]{1,2,0:T(2,128)(2,1)S(1)} all-to-all(bf16[32,4096,2]{1,2,0:T(2,128)(2,1)S(1)} %broadcast_in_dim.64), channel_id=1, replica_groups=mesh['pair_0'=4,'pair_1'=4,'pair_2'=2,'aux_0'=2,'aux_1'=2] {'pair_0','pa..., dimensions={0} | all-to-all | bytes 1048576 | tf_op jit(solution)/shard_map/all_to_all | solution.py:21
  551.2 30.6 %all_to_all.132 = f32[4,2048,64]{1,2,0:T(8,128)S(1)} all-to-all(f32[4,2048,64]{1,2,0:T(8,128)S(1)} %broadcast_in_dim.65), channel_id=1, replica_groups=mesh['pair_0'=4,'pair_1'=4,'pair_2'=2,'aux_0'=2,'aux_1'=2] {'aux_0','aux..., dimensions={0} | all-to-all | bytes 4194304 | tf_op jit(solution)/shard_map/all_to_all | solution.py:21
  591.4 20.9 %all_to_all.133 = f32[32,4096,2]{1,2,0:T(2,128)S(1)} all-to-all(f32[32,4096,2]{1,2,0:T(2,128)S(1)} %bitcast.113), channel_id=1, replica_groups=mesh['pair_0'=4,'pair_1'=4,'pair_2'=2,'aux_0'=2,'aux_1'=2] {'pair_0','pa..., dimensions={0} | all-to-all | bytes 2097152 | tf_op jit(solution)/shard_map/all_to_all | solution.py:36
  613.2 15.0 %all_to_all.134 = bf16[32,4096,2]{1,2,0:T(2,128)(2,1)S(1)} all-to-all(bf16[32,4096,2]{1,2,0:T(2,128)(2,1)S(1)} %broadcast_in_dim.66), channel_id=1, replica_groups=mesh['pair_0'=4,'pair_1'=4,'pair_2'=2,'aux_0'=2,'aux_1'=2] {'pair_0','pa..., dimensions={0} | all-to-all | bytes 1048576 | tf_op jit(solution)/shard_map/all_to_all | solution.py:21
  639.6 30.6 %all_to_all.135 = f32[4,2048,64]{1,2,0:T(8,128)S(1)} all-to-all(f32[4,2048,64]{1,2,0:T(8,128)S(1)} %broadcast_in_dim.67), channel_id=1, replica_groups=mesh['pair_0'=4,'pair_1'=4,'pair_2'=2,'aux_0'=2,'aux_1'=2] {'aux_0','aux..., dimensions={0} | all-to-all | bytes 4194304 | tf_op jit(solution)/shard_map/all_to_all | solution.py:21
  679.9 20.9 %all_to_all.136 = f32[32,4096,2]{1,2,0:T(2,128)S(1)} all-to-all(f32[32,4096,2]{1,2,0:T(2,128)S(1)} %bitcast.114), channel_id=1, replica_groups=mesh['pair_0'=4,'pair_1'=4,'pair_2'=2,'aux_0'=2,'aux_1'=2] {'pair_0','pa..., dimensions={0} | all-to-all | bytes 2097152 | tf_op jit(solution)/shard_map/all_to_all | solution.py:36
  (81 shorter events, 219.5 us)
Async XLA Ops:
  0.6 40.3 %copy-start = (f32[2048]{0:T(1024)S(1)}, f32[2048]{0:T(1024)}, u32[]{:S(2)}) copy-start(f32[2048]{0:T(1024)} %param.5) | copy-start | bytes 24580
  51.3 28.3 %all-to-all-start.1 = ((f32[32,4096,2]{1,2,0:T(2,128)}), f32[32,4096,2]{1,2,0:T(2,128)S(1)}, u32[]{:S(2)}, u32[]{:S(2)}) async-start(f32[32,4096,2]{1,2,0:T(2,128)} %bitcast.1), calls=%async_computation.1 | async-start | bytes 2097152 | tf_op jit(solution)/shard_map/all_to_all | solution.py:36
  670.2 72.1 %copy-start.1 = (f32[9]{0:T(128)S(1)}, f32[9]{0:T(128)}, u32[]{:S(2)}) copy-start(f32[9]{0:T(128)} %constant.33.clone) | copy-start | bytes 112
where the time goes:
time: 752 us; the launch traced here: 744 us
  blocking collectives  527 us (70%)
  matrix products  158 us (21%)
  local copies, waits for them, and re-layouts  18.1 us (2%)
  waiting for transfers between devices  17.8 us (2%)
  other arithmetic  10.5 us (1%)
  starting transfers between devices  10.4 us (1%)
    all_to_all x15, blocking collectives, sent_to_all(): return lax.all_to_all(copies, axis, split_axis=0, concat_axis=0, tiled=True)  348 us
    all_to_all x7, blocking collectives, summed_on_arrival(): lax.all_to_all(blocks, axis, split_axis=0, concat_axis=0, tiled=True)  146 us
    dot_general x8, matrix products, per_device(): rows = jnp.dot(pair_factors, gathered, preferred_element_type=jnp.float32)  87.9 us
    dot_general x8, matrix products, per_device(): lax.dot_general(pair_factors, scaled, (((0,), (0,)), ((), ())), preferred...  70.5 us
    psum x5, blocking collectives, by_axis(): return functools.reduce(lax.psum, axes, shard)  33.3 us
    all_to_all x1, waiting for transfers between devices, summed_on_arrival(): lax.all_to_all(blocks, axis, split_axis=0, concat_axis=0, tiled=True)  17.8 us
  transfers between devices with their start and end apart: 1, of which 1 were waited for; matrix products, arithmetic and copies ran while one was open for 0% of the time, Pallas kernels for 0%

commit v1 on v0

v1 whole, which is shorter than its diff:
```python
import jax
import jax.numpy as jnp
import numpy as np
from jax import lax
from jax.experimental import pallas as pl
from jax.experimental.pallas import tpu as pltpu
from jax.sharding import Mesh
from jax.sharding import PartitionSpec as P

ITERS = 8
AUX = ("aux_0", "aux_1")
PAIR = ("pair_0", "pair_1", "pair_2")
MESH_ID = pl.DeviceIdType.MESH
F32 = jnp.float32
BF16 = jnp.bfloat16

spread = 5.0

ROWS = 2048
COLS = 4096
NP = 64
HALF = 2
PEERS = 16
LANES = 128
NCH = 4
RCH = ROWS // NCH
RH = RCH // 2

OFFSETS = (
    (2, 2), (2, 1), (2, 3), (1, 2), (3, 2), (1, 1), (3, 3), (1, 3),
    (3, 1), (2, 0), (0, 2), (1, 0), (0, 1), (3, 0), (0, 3),
)


def cheb_coefficients(order_count):
    node_count = 64
    angles = (np.arange(node_count) + 0.5) * np.pi / node_count
    samples = np.log(1.0 + spread * (np.cos(angles) + 1.0) / 2.0)
    values = [
        2.0 / node_count * np.sum(samples * np.cos(degree * angles))
        for degree in range(order_count)
    ]
    values[0] = values[0] / 2.0
    return np.array(values)


def kernel(
    b_hbm, w_ref, z_hbm, out_ref, mom_out,
    bmat, bt, zbuf, vg, racc, own_half, asend, arecv, bsend, brecv, sbuf,
    rssend, rsrecv, xsend, xrecv, prob, prev, cur, finsend, finrecv, mom, momrecv, momx,
    load_sem, a_s, a_r, b_s, b_r, c_s, c_r, rs_s, rs_r, x_s, x_r, ag_s, ag_r, f_s, f_r, m_s, m_r, q_s, q_r,
):
    y = lax.axis_index("pair_0")
    z = lax.axis_index("pair_1")
    h = lax.axis_index("pair_2")
    xl = lax.axis_index("aux_0")
    core = lax.axis_index("aux_1")
    me = y * 4 + z

    def peer(dy, dz):
        return {"pair_0": lax.rem(y + dy, 4), "pair_1": lax.rem(z + dz, 4)}

    def peer_index(dy, dz):
        return lax.rem(y + dy, 4) * 4 + lax.rem(z + dz, 4)

    hi_id = {"pair_2": 1 - h}
    lo_id = {"aux_0": 1 - xl}
    core_id = {"aux_1": 1 - core}
    diag_id = {"aux_0": 1 - xl, "aux_1": 1 - core}

    loads = [
        pltpu.make_async_copy(
            b_hbm.at[pl.ds(r * 256, 256)], bmat.at[pl.ds(r * 256, 256)], load_sem.at[r]
        )
        for r in range(ROWS // 256)
    ]
    zload = pltpu.make_async_copy(z_hbm, zbuf, load_sem.at[ROWS // 256])
    zload.start()
    for ld in loads:
        ld.start()

    barrier = pltpu.get_barrier_semaphore()
    everyone = [peer(dy, dz) for dy, dz in OFFSETS] + [hi_id, lo_id, core_id, diag_id]
    for who in everyone:
        pl.semaphore_signal(barrier, inc=1, device_id=who, device_id_type=MESH_ID)

    def rcopy(src, dst, s, r, who):
        return pltpu.make_async_remote_copy(
            src_ref=src, dst_ref=dst, send_sem=s, recv_sem=r, device_id=who, device_id_type=MESH_ID
        )

    def wait_bytes(ref, sem):
        pltpu.make_async_copy(ref, ref, sem).wait()

    zload.wait()
    for c in range(HALF):
        def put(p, carry, c=c):
            blk = zbuf[pl.ds(c * 2048 + p * LANES, LANES), :]
            vg[c, p] = blk.T.astype(BF16)
            return carry
        lax.fori_loop(0, PEERS, put, 0)
        blk = zbuf[pl.ds(c * 2048 + me * LANES, LANES), :].T
        prob[c] = blk
        cur[c] = blk
        prev[c] = blk
    mom[...] = jnp.zeros_like(mom)
    mom[0:1, :] = jnp.sum(prob[0] * prob[0] + prob[1] * prob[1], axis=0, keepdims=True)

    for r in range(ROWS // 256):
        loads[r].wait()

        def flip(k, carry, r=r):
            bt[pl.ds(k * 256, 256), r * 256:(r + 1) * 256] = bmat[
                r * 256:(r + 1) * 256, pl.ds(k * 256, 256)
            ].T
            return carry

        lax.fori_loop(0, COLS // 256, flip, 0)

    pl.semaphore_wait(barrier, len(everyone))

    def vector(c):
        return jnp.concatenate([vg[c, p] for p in range(PEERS)], axis=1)

    def step(t, carry):
        par = lax.rem(t, 2)

        @pl.when(t > 0)
        def _():
            wait_bytes(vg.at[0, pl.ds(0, PEERS - 1)], ag_r.at[0])

        for i in range(NCH):
            racc[i] = jnp.dot(
                vector(0), bt[0:2048, i * RCH:(i + 1) * RCH], preferred_element_type=F32
            )

        @pl.when(t > 0)
        def _():
            wait_bytes(vg.at[1, pl.ds(0, PEERS - 1)], ag_r.at[1])
            for c in range(HALF):
                wait_bytes(vg.at[c, pl.ds(0, PEERS - 1)], ag_s.at[c])

        acopy = [
            rcopy(asend.at[i], arecv.at[i], a_s.at[i], a_r.at[i], core_id) for i in range(NCH)
        ]
        bcopy = [
            rcopy(bsend.at[i], brecv.at[par, i], b_s.at[i], b_r.at[par, i], lo_id)
            for i in range(NCH)
        ]
        ccopy = [
            rcopy(
                sbuf.at[2 * i + core], sbuf.at[2 * i + core], c_s.at[i], c_r.at[i], core_id
            )
            for i in range(NCH)
        ]

        def first(i):
            part = racc[i] + jnp.dot(
                vector(1), bt[2048:4096, i * RCH:(i + 1) * RCH], preferred_element_type=F32
            )
            low, high = part[:, :RH], part[:, RH:]
            own_half[i] = jnp.where(core == 0, low, high)
            asend[i] = jnp.where(core == 0, high, low).astype(BF16)
            acopy[i].start()

        def second(i):
            acopy[i].wait_recv()
            bsend[i] = (own_half[i] + arecv[i].astype(F32)).astype(BF16)
            bcopy[i].start()

        def third(i):
            bcopy[i].wait_recv()
            total = bsend[i].astype(F32) + brecv[par, i].astype(F32)
            sbuf[2 * i + core] = (w_ref[2 * i + core] * total).astype(BF16)
            ccopy[i].start()

        first(0)
        first(1)
        first(2)
        second(0)
        first(3)
        second(1)
        second(2)
        second(3)
        for i in range(NCH):
            third(i)
        for i in range(NCH):
            ccopy[i].wait_recv()
            acopy[i].wait_send()
            bcopy[i].wait_send()
            ccopy[i].wait_send()

        scaled = lambda: jnp.concatenate([sbuf[q] for q in range(2 * NCH)], axis=1)
        for c in range(HALF):
            for n in range(4):
                col = c * 2048 + n * 512
                img = jnp.dot(
                    scaled(), bmat[:, col:col + 512], preferred_element_type=F32
                ).astype(BF16)
                for q in range(4):
                    rssend[c, n * 4 + q] = img[:, q * LANES:(q + 1) * LANES]
            for dy, dz in OFFSETS:
                rcopy(
                    rssend.at[c, peer_index(dy, dz)], rsrecv.at[c, me],
                    rs_s.at[c], rs_r.at[c], peer(dy, dz),
                ).start()
            rsrecv[c, me] = rssend[c, me]

        xcopy = [
            rcopy(xsend.at[c], xrecv.at[par, c], x_s.at[c], x_r.at[par, c], hi_id)
            for c in range(HALF)
        ]
        for c in range(HALF):
            wait_bytes(rsrecv.at[c, pl.ds(0, PEERS - 1)], rs_r.at[c])
            total = rsrecv[c, 0].astype(F32)
            for p in range(1, PEERS):
                total = total + rsrecv[c, p].astype(F32)
            xsend[c] = total.astype(BF16)
            xcopy[c].start()

        gain = jnp.where(t == 0, 1.0, 2.0).astype(F32)
        back = jnp.where(t == 0, 0.0, 1.0).astype(F32)
        for c in range(HALF):
            xcopy[c].wait_recv()
            image = xsend[c].astype(F32) + xrecv[par, c].astype(F32)
            now = cur[c]
            mapped = (2.0 / spread) * image - now
            following = gain * mapped - back * prev[c]
            prev[c] = now
            cur[c] = following

            @pl.when(t < ITERS - 1)
            def _(c=c, following=following):
                vg[c, me] = following.astype(BF16)
                for dy, dz in OFFSETS:
                    rcopy(
                        vg.at[c, me], vg.at[c, me], ag_s.at[c], ag_r.at[c], peer(dy, dz)
                    ).start()

        mom[pl.ds(t + 1, 1), :] = jnp.sum(
            prob[0] * cur[0] + prob[1] * cur[1], axis=0, keepdims=True
        )
        for c in range(HALF):
            xcopy[c].wait_send()
            wait_bytes(rssend.at[c, pl.ds(0, PEERS - 1)], rs_s.at[c])
        return carry

    lax.fori_loop(0, ITERS, step, 0)

    momrecv[me] = mom[...]
    for dy, dz in OFFSETS:
        rcopy(mom, momrecv.at[me], m_s, m_r, peer(dy, dz)).start()
    for p in range(PEERS):
        for c in range(HALF):
            four = cur[c, 4 * p:4 * p + 4, :]
            finsend[p, 2 * c:2 * c + 2, :] = jnp.where(h == 0, four[0:2], four[2:4])
    for dy, dz in OFFSETS:
        rcopy(finsend.at[peer_index(dy, dz)], finrecv.at[me], f_s, f_r, peer(dy, dz)).start()
    finrecv[me] = finsend[me]

    wait_bytes(momrecv.at[pl.ds(0, PEERS - 1)], m_r)
    total = momrecv[0]
    for p in range(1, PEERS):
        total = total + momrecv[p]
    slot = xl * 2 + core
    momx[slot] = total
    for who in (core_id, lo_id, diag_id):
        rcopy(momx.at[slot], momx.at[slot], q_s, q_r, who).start()
    wait_bytes(finrecv.at[pl.ds(0, PEERS - 1)], f_r)
    out_ref[...] = finrecv[...]
    wait_bytes(momx.at[pl.ds(0, 3)], q_r)
    mom_out[...] = (momx[0] + momx[1]) + (momx[2] + momx[3])
    wait_bytes(momrecv.at[pl.ds(0, PEERS - 1)], m_s)
    wait_bytes(finsend.at[pl.ds(0, PEERS - 1)], f_s)
    wait_bytes(momx.at[pl.ds(0, 3)], q_s)


def per_device(pair_factors, pair_weights, probes):
    vm = pltpu.VMEM
    dma = pltpu.SemaphoreType.DMA
    out, mom = pl.pallas_call(
        kernel,
        out_shape=(
            jax.ShapeDtypeStruct((PEERS, 4, LANES), F32),
            jax.ShapeDtypeStruct((16, LANES), F32),
        ),
        in_specs=[
            pl.BlockSpec(memory_space=pl.ANY),
            pl.BlockSpec(memory_space=pltpu.VMEM),
            pl.BlockSpec(memory_space=pl.ANY),
        ],
        out_specs=(
            pl.BlockSpec(memory_space=pltpu.VMEM),
            pl.BlockSpec(memory_space=pltpu.VMEM),
        ),
        scratch_shapes=[
            vm((ROWS, COLS), BF16),
            vm((COLS, ROWS), BF16),
            vm((COLS, NP), F32),
            vm((HALF, PEERS, NP, LANES), BF16),
            vm((NCH, NP, RCH), F32),
            vm((NCH, NP, RH), F32),
            vm((NCH, NP, RH), BF16),
            vm((NCH, NP, RH), BF16),
            vm((NCH, NP, RH), BF16),
            vm((2, NCH, NP, RH), BF16),
            vm((2 * NCH, NP, RH), BF16),
            vm((HALF, PEERS, NP, LANES), BF16),
            vm((HALF, PEERS, NP, LANES), BF16),
            vm((HALF, NP, LANES), BF16),
            vm((2, HALF, NP, LANES), BF16),
            vm((HALF, NP, LANES), F32),
            vm((HALF, NP, LANES), F32),
            vm((HALF, NP, LANES), F32),
            vm((PEERS, 4, LANES), F32),
            vm((PEERS, 4, LANES), F32),
            vm((16, LANES), F32),
            vm((PEERS, 16, LANES), F32),
            vm((4, 16, LANES), F32),
            dma((ROWS // 256 + 1,)),
            dma((NCH,)), dma((NCH,)),
            dma((NCH,)), dma((2, NCH)),
            dma((NCH,)), dma((NCH,)),
            dma((HALF,)), dma((HALF,)),
            dma((HALF,)), dma((2, HALF)),
            dma((HALF,)), dma((HALF,)),
            dma, dma, dma, dma, dma, dma,
        ],
        compiler_params=pltpu.CompilerParams(
            collective_id=0, has_side_effects=True, vmem_limit_bytes=60 * 1024 * 1024
        ),
        name="cheb",
    )(pair_factors, pair_weights.reshape(2 * NCH, 1, RH), probes)
    own = out.reshape(PEERS, HALF, 2, LANES).transpose(1, 0, 3, 2).reshape(COLS, 2)
    divisor = NP * COLS * lax.axis_size(AUX)
    moments = jnp.sum(mom, axis=1)[: ITERS + 1] / divisor
    coefficients = jnp.asarray(cheb_coefficients(ITERS + 1)).astype(moments.dtype)
    energy = jnp.sum(coefficients * moments).reshape(1)
    return (own, moments, energy)


def solution(mesh):
    torus = Mesh(
        mesh.devices.reshape(4, 4, 2, 2, 2), ("pair_0", "pair_1", "pair_2", "aux_0", "aux_1")
    )
    return jax.shard_map(
        per_device,
        mesh=torus,
        in_specs=(P(PAIR, AUX), P(PAIR), P(AUX, None)),
        out_specs=(P(AUX, PAIR), P(), P()),
        check_vma=False,
    )
```

time: 752 us -> 252 us (0.34)
  blocking collectives: 527 us -> 0 us
  Pallas kernels: 0 us -> 244 us
  matrix products: 158 us -> 0 us
  waiting for transfers between devices: 17.8 us -> 0 us
  local copies, waits for them, and re-layouts: 18.1 us -> 4.6 us
  starting transfers between devices: 10.4 us -> 0 us
  other arithmetic: 10.5 us -> 1.92 us
    all_to_all x22 -> x0, blocking collectives: 494 us -> none  [the longest x15 348 us: sent_to_all(): return lax.all_to_all(copies, axis, split_axis=0, concat_axis=0, tiled=True)]
    pallas_call x0 -> x1, Pallas kernels: none -> 244 us  [per_device(): pl.pallas_call(kernel, out_shape=(jax.ShapeDtypeStruct((PEERS, 4, LANES),...]
    dot_general x16 -> x0, matrix products: 158 us -> none  [the longest x8 87.9 us: per_device(): rows = jnp.dot(pair_factors, gathered, preferred_element_type=jnp.float32)]
    psum x5 -> x0, blocking collectives: 33.3 us -> none  [by_axis(): return functools.reduce(lax.psum, axes, shard)]
    all_to_all x1 -> x0, waiting for transfers between devices: 17.8 us -> none  [summed_on_arrival(): lax.all_to_all(blocks, axis, split_axis=0, concat_axis=0, tiled=True)]
    all_to_all x1 -> x0, starting transfers between devices: 10.4 us -> none  [summed_on_arrival(): lax.all_to_all(blocks, axis, split_axis=0, concat_axis=0, tiled=True)]
  transfers between devices with their start and end apart: 1 -> 0, of which waited for: 1 -> 0; matrix products, arithmetic and copies ran while one was open for 0% -> 0% of each run, Pallas kernels for 0% -> 0%
where the time goes in v1:
time: 252 us; the launch traced here: 251 us
  Pallas kernels  244 us (97%)
  local copies, waits for them, and re-layouts  4.6 us (2%)
    pallas_call x1, Pallas kernels, per_device(): pl.pallas_call(kernel, out_shape=(jax.ShapeDtypeStruct((PEERS, 4, LANES),...  244 us

profile of v1, /device:TPU:1, one launch (start us, length us, event | category | flops | bytes accessed | tf_op | source)
XLA Modules:
  0.0 251.3 jit_solution(6356781379934814105)
XLA Ops:
  0.6 0.0 copy-start
  0.6 3.2 %copy.7.z_hbm = f32[4096,64]{1,0:T(8,128)} copy(f32[4096,64]{0,1:T(8,128)} %param.6) | data formatting | bytes 2097152 | tf_op args[2]
  3.8 244.1 %cheb.1 = (f32[16,4,128]{2,1,0:T(4,128)}, f32[16,128]{1,0:T(8,128)}) custom-call(bf16[2048,4096]{1,0:T(8,128)(2,1)} %b_hbm.1, f32[8,1,256]{2,1,0:T(1,128)} %bitcast.15, f32[4096,64]{1,0:T(8,128)} %copy.7.z_hbm), custom_call_target="tpu_custom_call" | custom-call | tf_op jit(solution)/shard_map/cheb/pallas_call | solution.py:281
  248.0 0.8 copy.8
  248.7 0.6 copy.11
  249.4 0.8 reduce_sum.18
  250.2 0.0 copy-done
  250.2 1.1 multiply_reduce_fusion
Async XLA Ops:
  0.6 249.6 %copy-start = (f32[9]{0:T(128)S(1)}, f32[9]{0:T(128)}, u32[]{:S(2)}) copy-start(f32[9]{0:T(128)} %constant.7.clone) | copy-start | bytes 112

commit v2 on v1

v2 whole, which is shorter than its diff:
```python
import jax
import jax.numpy as jnp
import numpy as np
from jax import lax
from jax.experimental import pallas as pl
from jax.experimental.pallas import tpu as pltpu
from jax.sharding import Mesh
from jax.sharding import PartitionSpec as P

ITERS = 8
AUX = ("aux_0", "aux_1")
PAIR = ("pair_0", "pair_1", "pair_2")
MESH_ID = pl.DeviceIdType.MESH
F32 = jnp.float32
BF16 = jnp.bfloat16

spread = 5.0

ROWS = 2048
COLS = 4096
NP = 64
CH = 4
WIDE = COLS // CH
TILES = WIDE // 128
PR = NP // 2
PEERS = 16
LANES = 128
NCH = 4
RCH = ROWS // NCH
RH = RCH // 2

OFFSETS = (
    (2, 2), (2, 1), (2, 3), (1, 2), (3, 2), (1, 1), (3, 3), (1, 3),
    (3, 1), (2, 0), (0, 2), (1, 0), (0, 1), (3, 0), (0, 3),
)

FAR = ((0, 2), (0, 1), (0, 3), (1, 2), (0, 0), (1, 1), (1, 3), (1, 0))
NEAR = ((1, 2), (1, 1), (1, 3), (0, 2), (1, 0), (0, 1), (0, 3))


def cheb_coefficients(order_count):
    node_count = 64
    angles = (np.arange(node_count) + 0.5) * np.pi / node_count
    samples = np.log(1.0 + spread * (np.cos(angles) + 1.0) / 2.0)
    values = [
        2.0 / node_count * np.sum(samples * np.cos(degree * angles))
        for degree in range(order_count)
    ]
    values[0] = values[0] / 2.0
    return np.array(values)


def kernel(
    b_hbm, w_ref, z_hbm, out_ref, mom_out, energy_out,
    bmat, bt, zbuf, vg, racc, own_half, asend, arecv, bsend, brecv, sbuf,
    rssend, rsrecv, xsend, xrecv, prob, prev, cur, finsend, finrecv, mom, momrecv, momx,
    load_sem, a_s, a_r, b_s, b_r, c_s, c_r, rs_s, rs_r, x_s, x_r, ag_s, ag_r, f_s, f_r, m_s, m_r, q_s, q_r,
):
    y = lax.axis_index("pair_0")
    z = lax.axis_index("pair_1")
    h = lax.axis_index("pair_2")
    xl = lax.axis_index("aux_0")
    core = lax.axis_index("aux_1")
    me = y * 4 + z

    def peer(dy, dz):
        return {"pair_0": lax.rem(y + dy, 4), "pair_1": lax.rem(z + dz, 4)}

    def peer_index(dy, dz):
        return lax.rem(y + dy, 4) * 4 + lax.rem(z + dz, 4)

    hi_id = {"pair_2": 1 - h}
    lo_id = {"aux_0": 1 - xl}
    core_id = {"aux_1": 1 - core}
    diag_id = {"aux_0": 1 - xl, "aux_1": 1 - core}

    loads = [
        pltpu.make_async_copy(
            b_hbm.at[pl.ds(r * 256, 256)], bmat.at[pl.ds(r * 256, 256)], load_sem.at[r]
        )
        for r in range(ROWS // 256)
    ]
    zload = pltpu.make_async_copy(z_hbm, zbuf, load_sem.at[ROWS // 256])
    loads[0].start()
    zload.start()
    for ld in loads[1:]:
        ld.start()

    barrier = pltpu.get_barrier_semaphore()
    everyone = [peer(dy, dz) for dy, dz in OFFSETS] + [hi_id, lo_id, core_id, diag_id]
    for who in everyone:
        pl.semaphore_signal(barrier, inc=1, device_id=who, device_id_type=MESH_ID)

    def rcopy(src, dst, s, r, who):
        return pltpu.make_async_remote_copy(
            src_ref=src, dst_ref=dst, send_sem=s, recv_sem=r, device_id=who, device_id_type=MESH_ID
        )

    def wait_bytes(ref, sem):
        pltpu.make_async_copy(ref, ref, sem).wait()

    def flip_rows(r):
        loads[r].wait()

        def flip(k, carry):
            bt[pl.ds(k * 256, 256), r * 256:(r + 1) * 256] = bmat[
                r * 256:(r + 1) * 256, pl.ds(k * 256, 256)
            ].T
            return carry

        lax.fori_loop(0, COLS // 256, flip, 0)

    flip_rows(0)
    zload.wait()
    for j in range(CH):
        for p in range(PEERS):
            col = (j * TILES + p // 2) * LANES
            vg[j, p] = zbuf[PR * (p % 2):PR * (p % 2) + PR, col:col + LANES].astype(BF16)
        blk = zbuf[
            pl.ds(pl.multiple_of(PR * lax.rem(me, 2), PR), PR),
            pl.ds(pl.multiple_of((j * TILES + me // 2) * LANES, LANES), LANES),
        ]
        prob[j] = blk
        cur[j] = blk
        prev[j] = blk

    def dots():
        acc = prob[0] * cur[0]
        for j in range(1, CH):
            acc = acc + prob[j] * cur[j]
        return jnp.sum(acc, axis=0, keepdims=True)

    mom[...] = jnp.zeros_like(mom)
    mom[0:1, :] = dots()
    for r in range(1, ROWS // 256):
        flip_rows(r)

    pl.semaphore_wait(barrier, len(everyone))

    def vector(j):
        return jnp.concatenate(
            [
                jnp.concatenate([vg[j, 2 * k], vg[j, 2 * k + 1]], axis=0)
                for k in range(TILES)
            ],
            axis=1,
        )

    def step(t, carry):
        par = lax.rem(t, 2)

        def rows_part(j, i):
            return jnp.dot(
                vector(j),
                bt[j * WIDE:(j + 1) * WIDE, i * RCH:(i + 1) * RCH],
                preferred_element_type=F32,
            )

        for j in range(CH):
            @pl.when(t > 0)
            def _(j=j):
                wait_bytes(vg.at[j, pl.ds(0, PEERS - 1)], ag_r.at[j])

            if j == CH - 1:
                break
            for i in range(NCH):
                part = rows_part(j, i)
                racc[i] = part if j == 0 else racc[i] + part

        acopy = [
            rcopy(asend.at[i], arecv.at[i], a_s.at[i], a_r.at[i], core_id) for i in range(NCH)
        ]
        bcopy = [
            rcopy(bsend.at[i], brecv.at[par, i], b_s.at[i], b_r.at[par, i], lo_id)
            for i in range(NCH)
        ]
        ccopy = [
            rcopy(
                sbuf.at[2 * i + core], sbuf.at[2 * i + core], c_s.at[i], c_r.at[i], core_id
            )
            for i in range(NCH)
        ]

        def first(i):
            part = racc[i] + rows_part(CH - 1, i)
            low, high = part[:, :RH], part[:, RH:]
            own_half[i] = jnp.where(core == 0, low, high)
            asend[i] = jnp.where(core == 0, high, low).astype(BF16)
            acopy[i].start()

        def second(i):
            acopy[i].wait_recv()
            bsend[i] = (own_half[i] + arecv[i].astype(F32)).astype(BF16)
            bcopy[i].start()

        def third(i):
            bcopy[i].wait_recv()
            total = bsend[i].astype(F32) + brecv[par, i].astype(F32)
            sbuf[2 * i + core] = (w_ref[2 * i + core] * total).astype(BF16)
            ccopy[i].start()

        for i in range(NCH):
            first(i)
        for i in range(NCH):
            second(i)

        @pl.when(t > 0)
        def _():
            for j in range(CH):
                wait_bytes(vg.at[j, pl.ds(0, PEERS - 1)], ag_s.at[j])

        for i in range(NCH):
            third(i)
        for i in range(NCH):
            ccopy[i].wait_recv()

        def scaled():
            return jnp.concatenate([sbuf[q] for q in range(2 * NCH)], axis=1)

        far = 1 - y // 2
        for j in range(CH):
            for k in range(2):
                side = far if k == 0 else 1 - far
                col = pl.multiple_of(j * WIDE + side * 512, 512)
                img = jnp.dot(
                    scaled(), bmat[:, pl.ds(col, 512)], preferred_element_type=F32
                ).astype(BF16)
                for q in range(4):
                    for g in range(2):
                        rssend[j, side * 8 + 2 * q + g] = img[
                            g * PR:(g + 1) * PR, q * LANES:(q + 1) * LANES
                        ]
                order = FAR if k == 0 else NEAR
                for dy, dz in order:
                    ty = 2 * side + lax.rem(y + dy, 2)
                    tz = lax.rem(z + dz, 4)
                    rcopy(
                        rssend.at[j, ty * 4 + tz], rsrecv.at[j, me],
                        rs_s.at[j], rs_r.at[j], {"pair_0": ty, "pair_1": tz},
                    ).start()
            rsrecv[j, me] = rssend[j, me]

        for i in range(NCH):
            acopy[i].wait_send()
            bcopy[i].wait_send()
            ccopy[i].wait_send()

        xcopy = [
            rcopy(xsend.at[j], xrecv.at[par, j], x_s.at[j], x_r.at[par, j], hi_id)
            for j in range(CH)
        ]
        for j in range(CH):
            wait_bytes(rsrecv.at[j, pl.ds(0, PEERS - 1)], rs_r.at[j])
            total = rsrecv[j, 0].astype(F32)
            for p in range(1, PEERS):
                total = total + rsrecv[j, p].astype(F32)
            xsend[j] = total.astype(BF16)
            xcopy[j].start()

        gain = jnp.where(t == 0, 1.0, 2.0).astype(F32)
        back = jnp.where(t == 0, 0.0, 1.0).astype(F32)
        for j in range(CH):
            xcopy[j].wait_recv()
            image = xsend[j].astype(F32) + xrecv[par, j].astype(F32)
            now = cur[j]
            mapped = (2.0 / spread) * image - now
            following = gain * mapped - back * prev[j]
            prev[j] = now
            cur[j] = following

            @pl.when(t < ITERS - 1)
            def _(j=j, following=following):
                vg[j, me] = following.astype(BF16)
                for dy, dz in OFFSETS:
                    rcopy(
                        vg.at[j, me], vg.at[j, me], ag_s.at[j], ag_r.at[j], peer(dy, dz)
                    ).start()

        mom[pl.ds(t + 1, 1), :] = dots()
        for j in range(CH):
            xcopy[j].wait_send()
            wait_bytes(rssend.at[j, pl.ds(0, PEERS - 1)], rs_s.at[j])
        return carry

    lax.fori_loop(0, ITERS, step, 0)

    momrecv[me] = mom[...]
    for dy, dz in OFFSETS:
        rcopy(mom, momrecv.at[me], m_s, m_r, peer(dy, dz)).start()
    for q in range(8):
        for j in range(CH):
            four = cur[j, 4 * q:4 * q + 4, :]
            finsend[q, 2 * j:2 * j + 2, :] = jnp.where(h == 0, four[0:2], four[2:4])
    for dy, dz in OFFSETS:
        rcopy(
            finsend.at[lax.rem(peer_index(dy, dz), 8)], finrecv.at[me], f_s, f_r, peer(dy, dz)
        ).start()
    finrecv[me] = finsend[lax.rem(me, 8)]

    wait_bytes(momrecv.at[pl.ds(0, PEERS - 1)], m_r)
    total = momrecv[0]
    for p in range(1, PEERS):
        total = total + momrecv[p]
    slot = xl * 2 + core
    momx[slot] = total
    for who in (core_id, lo_id, diag_id):
        rcopy(momx.at[slot], momx.at[slot], q_s, q_r, who).start()
    wait_bytes(finrecv.at[pl.ds(0, PEERS - 1)], f_r)
    half = me // 8
    for k in range(TILES):
        for j in range(CH):
            col = (j * TILES + k) * LANES
            out_ref[:, col:col + LANES] = finrecv[2 * k + half, 2 * j:2 * j + 2, :]
    wait_bytes(momx.at[pl.ds(0, 3)], q_r)
    moments = jnp.sum(
        (momx[0] + momx[1]) + (momx[2] + momx[3]), axis=1, keepdims=True
    ) * (1.0 / (NP * COLS * 4))
    energy = jnp.zeros((), F32)
    for k, c in enumerate(cheb_coefficients(ITERS + 1)):
        mom_out[k] = moments[k, 0]
        energy = energy + moments[k, 0] * float(c)
    energy_out[0] = energy
    wait_bytes(momrecv.at[pl.ds(0, PEERS - 1)], m_s)
    wait_bytes(finrecv.at[pl.ds(0, PEERS - 1)], f_s)
    wait_bytes(momx.at[pl.ds(0, 3)], q_s)


def per_device(pair_factors, pair_weights, probes):
    vm = pltpu.VMEM
    dma = pltpu.SemaphoreType.DMA
    out, moments, energy = pl.pallas_call(
        kernel,
        out_shape=(
            jax.ShapeDtypeStruct((2, COLS), F32),
            jax.ShapeDtypeStruct((ITERS + 1,), F32),
            jax.ShapeDtypeStruct((1,), F32),
        ),
        in_specs=[
            pl.BlockSpec(memory_space=pl.ANY),
            pl.BlockSpec(memory_space=pltpu.VMEM),
            pl.BlockSpec(memory_space=pl.ANY),
        ],
        out_specs=(
            pl.BlockSpec(memory_space=pltpu.VMEM),
            pl.BlockSpec(memory_space=pltpu.SMEM),
            pl.BlockSpec(memory_space=pltpu.SMEM),
        ),
        scratch_shapes=[
            vm((ROWS, COLS), BF16),
            vm((COLS, ROWS), BF16),
            vm((NP, COLS), F32),
            vm((CH, PEERS, PR, LANES), BF16),
            vm((NCH, NP, RCH), F32),
            vm((NCH, NP, RH), F32),
            vm((NCH, NP, RH), BF16),
            vm((NCH, NP, RH), BF16),
            vm((NCH, NP, RH), BF16),
            vm((2, NCH, NP, RH), BF16),
            vm((2 * NCH, NP, RH), BF16),
            vm((CH, PEERS, PR, LANES), BF16),
            vm((CH, PEERS, PR, LANES), BF16),
            vm((CH, PR, LANES), BF16),
            vm((2, CH, PR, LANES), BF16),
            vm((CH, PR, LANES), F32),
            vm((CH, PR, LANES), F32),
            vm((CH, PR, LANES), F32),
            vm((8, 2 * CH, LANES), F32),
            vm((PEERS, 2 * CH, LANES), F32),
            vm((16, LANES), F32),
            vm((PEERS, 16, LANES), F32),
            vm((4, 16, LANES), F32),
            dma((ROWS // 256 + 1,)),
            dma((NCH,)), dma((NCH,)),
            dma((NCH,)), dma((2, NCH)),
            dma((NCH,)), dma((NCH,)),
            dma((CH,)), dma((CH,)),
            dma((CH,)), dma((2, CH)),
            dma((CH,)), dma((CH,)),
            dma, dma, dma, dma, dma, dma,
        ],
        compiler_params=pltpu.CompilerParams(
            collective_id=0, has_side_effects=True, vmem_limit_bytes=60 * 1024 * 1024
        ),
        name="cheb",
    )(pair_factors, pair_weights.reshape(2 * NCH, 1, RH), probes.T)
    return (out.T, moments, energy)


def solution(mesh):
    torus = Mesh(
        mesh.devices.reshape(4, 4, 2, 2, 2), ("pair_0", "pair_1", "pair_2", "aux_0", "aux_1")
    )
    return jax.shard_map(
        per_device,
        mesh=torus,
        in_specs=(P(PAIR, AUX), P(PAIR), P(AUX, None)),
        out_specs=(P(AUX, PAIR), P(), P()),
        check_vma=False,
    )
```

time: 252 us -> 235 us (0.933)
  Pallas kernels: 244 us -> 230 us
    pallas_call x1, Pallas kernels: 244 us -> 230 us  [per_device(): pl.pallas_call(kernel, out_shape=(jax.ShapeDtypeStruct((2, COLS), F32), j...]
where the time goes in v2:
time: 235 us
  Pallas kernels  230 us (98%)
  local copies, waits for them, and re-layouts  2.55 us (1%)
  between operations  2.38 us (1%)
    pallas_call x1, Pallas kernels, per_device(): pl.pallas_call(kernel, out_shape=(jax.ShapeDtypeStruct((2, COLS), F32), j...  230 us

profile of v2, /device:TPU:1, one launch (start us, length us, event | category | flops | bytes accessed | tf_op | source)
XLA Modules:
  0.0 234.9 jit_solution(1193490319404201098)
XLA Ops:
  0.6 230.0 %cheb.1 = (f32[2,4096]{1,0:T(2,128)}, f32[9]{0:T(128)}, f32[1]{0:T(128)}) custom-call(bf16[2048,4096]{1,0:T(8,128)(2,1)} %b_hbm.1, f32[8,1,256]{2,1,0:T(1,128)} %bitcast.5, f32[64,4096]{1,0:T(8,128)} %bitcast.3), custom_call_target="tpu_custom_call" | custom-call | tf_op jit(solution)/shard_map/cheb/pallas_call | solution.py:331
  230.6 1.4 copy.9
  232.0 1.2 copy.10

commit v3 on v2

--- a/solution.py
+++ b/solution.py
@@ -19,23 +19,24 @@
 ROWS = 2048
 COLS = 4096
 NP = 64
-CH = 4
+CH = 2
 WIDE = COLS // CH
 TILES = WIDE // 128
-PR = NP // 2
-PEERS = 16
+OWNERS = 32
+PARTS = OWNERS // TILES
+PR = NP // PARTS
+PEERS = 32
 LANES = 128
 NCH = 4
 RCH = ROWS // NCH
 RH = RCH // 2
 
-OFFSETS = (
+PLANE = (
     (2, 2), (2, 1), (2, 3), (1, 2), (3, 2), (1, 1), (3, 3), (1, 3),
-    (3, 1), (2, 0), (0, 2), (1, 0), (0, 1), (3, 0), (0, 3),
+    (3, 1), (2, 0), (0, 2), (1, 0), (0, 1), (3, 0), (0, 3), (0, 0),
 )
-
-FAR = ((0, 2), (0, 1), (0, 3), (1, 2), (0, 0), (1, 1), (1, 3), (1, 0))
-NEAR = ((1, 2), (1, 1), (1, 3), (0, 2), (1, 0), (0, 1), (0, 3))
+OFFSETS = tuple((dy, dz, 1) for dy, dz in PLANE) + tuple((dy, dz, 0) for dy, dz in PLANE[:-1])
+ZH = ((2, 1), (1, 1), (3, 1), (2, 0), (0, 1), (1, 0), (3, 0), (0, 0))
 
 
 def cheb_coefficients(order_count):
@@ -53,23 +54,24 @@
 def kernel(
     b_hbm, w_ref, z_hbm, out_ref, mom_out, energy_out,
     bmat, bt, zbuf, vg, racc, own_half, asend, arecv, bsend, brecv, sbuf,
-    rssend, rsrecv, xsend, xrecv, prob, prev, cur, finsend, finrecv, mom, momrecv, momx,
-    load_sem, a_s, a_r, b_s, b_r, c_s, c_r, rs_s, rs_r, x_s, x_r, ag_s, ag_r, f_s, f_r, m_s, m_r, q_s, q_r,
+    rssend, rsrecv, prob, prev, cur, finsend, finrecv, mom, momrecv, momx,
+    load_sem, a_s, a_r, b_s, b_r, c_s, c_r, rs_s, rs_r, ag_s, ag_r, f_s, f_r, m_s, m_r, q_s, q_r,
 ):
     y = lax.axis_index("pair_0")
     z = lax.axis_index("pair_1")
     h = lax.axis_index("pair_2")
     xl = lax.axis_index("aux_0")
     core = lax.axis_index("aux_1")
-    me = y * 4 + z
-
-    def peer(dy, dz):
-        return {"pair_0": lax.rem(y + dy, 4), "pair_1": lax.rem(z + dz, 4)}
-
-    def peer_index(dy, dz):
-        return lax.rem(y + dy, 4) * 4 + lax.rem(z + dz, 4)
-
-    hi_id = {"pair_2": 1 - h}
+    me = (y * 4 + z) * 2 + h
+
+    def peer(dy, dz, dh):
+        return {
+            "pair_0": lax.rem(y + dy, 4), "pair_1": lax.rem(z + dz, 4), "pair_2": lax.rem(h + dh, 2)
+        }
+
+    def peer_index(dy, dz, dh):
+        return (lax.rem(y + dy, 4) * 4 + lax.rem(z + dz, 4)) * 2 + lax.rem(h + dh, 2)
+
     lo_id = {"aux_0": 1 - xl}
     core_id = {"aux_1": 1 - core}
     diag_id = {"aux_0": 1 - xl, "aux_1": 1 - core}
@@ -87,7 +89,7 @@
         ld.start()
 
     barrier = pltpu.get_barrier_semaphore()
-    everyone = [peer(dy, dz) for dy, dz in OFFSETS] + [hi_id, lo_id, core_id, diag_id]
+    everyone = [peer(*off) for off in OFFSETS] + [lo_id, core_id, diag_id]
     for who in everyone:
         pl.semaphore_signal(barrier, inc=1, device_id=who, device_id_type=MESH_ID)
 
@@ -114,11 +116,12 @@
     zload.wait()
     for j in range(CH):
         for p in range(PEERS):
-            col = (j * TILES + p // 2) * LANES
-            vg[j, p] = zbuf[PR * (p % 2):PR * (p % 2) + PR, col:col + LANES].astype(BF16)
+            col = (j * TILES + p // PARTS) * LANES
+            row = PR * (p % PARTS)
+            vg[j, p] = zbuf[row:row + PR, col:col + LANES].astype(BF16)
         blk = zbuf[
-            pl.ds(pl.multiple_of(PR * lax.rem(me, 2), PR), PR),
-            pl.ds(pl.multiple_of((j * TILES + me // 2) * LANES, LANES), LANES),
+            pl.ds(pl.multiple_of(PR * lax.rem(me, PARTS), PR), PR),
+            pl.ds(pl.multiple_of((j * TILES + me // PARTS) * LANES, LANES), LANES),
         ]
         prob[j] = blk
         cur[j] = blk
@@ -140,7 +143,7 @@
     def vector(j):
         return jnp.concatenate(
             [
-                jnp.concatenate([vg[j, 2 * k], vg[j, 2 * k + 1]], axis=0)
+                jnp.concatenate([vg[j, PARTS * k + g] for g in range(PARTS)], axis=0)
                 for k in range(TILES)
             ],
             axis=1,
@@ -217,27 +220,34 @@
         def scaled():
             return jnp.concatenate([sbuf[q] for q in range(2 * NCH)], axis=1)
 
-        far = 1 - y // 2
-        for j in range(CH):
-            for k in range(2):
-                side = far if k == 0 else 1 - far
+        for j in range(CH):
+            for k in range(TILES // 4):
+                if CH == 2:
+                    side = lax.rem(y + (2, 1, 3, 0)[k], 4)
+                    ys = [side]
+                else:
+                    side = (1 - y // 2) if k == 0 else y // 2
+                    low = lax.rem(y, 2)
+                    ys = [2 * side + low, 2 * side + 1 - low]
+                    ys = ys if k == 0 else ys[::-1]
                 col = pl.multiple_of(j * WIDE + side * 512, 512)
                 img = jnp.dot(
                     scaled(), bmat[:, pl.ds(col, 512)], preferred_element_type=F32
                 ).astype(BF16)
                 for q in range(4):
-                    for g in range(2):
-                        rssend[j, side * 8 + 2 * q + g] = img[
+                    for g in range(PARTS):
+                        rssend[j, (side * 4 + q) * PARTS + g] = img[
                             g * PR:(g + 1) * PR, q * LANES:(q + 1) * LANES
                         ]
-                order = FAR if k == 0 else NEAR
-                for dy, dz in order:
-                    ty = 2 * side + lax.rem(y + dy, 2)
-                    tz = lax.rem(z + dz, 4)
-                    rcopy(
-                        rssend.at[j, ty * 4 + tz], rsrecv.at[j, me],
-                        rs_s.at[j], rs_r.at[j], {"pair_0": ty, "pair_1": tz},
-                    ).start()
+                for m, ty in enumerate(ys):
+                    own = k == TILES // 4 - 1 and m == len(ys) - 1
+                    for dz, dh in ZH[:7] if own else ZH:
+                        tz = lax.rem(z + dz, 4)
+                        th = lax.rem(h + dh, 2)
+                        rcopy(
+                            rssend.at[j, (ty * 4 + tz) * 2 + th], rsrecv.at[j, me],
+                            rs_s.at[j], rs_r.at[j], {"pair_0": ty, "pair_1": tz, "pair_2": th},
+                        ).start()
             rsrecv[j, me] = rssend[j, me]
 
         for i in range(NCH):
@@ -245,23 +255,13 @@
             bcopy[i].wait_send()
             ccopy[i].wait_send()
 
-        xcopy = [
-            rcopy(xsend.at[j], xrecv.at[par, j], x_s.at[j], x_r.at[par, j], hi_id)
-            for j in range(CH)
-        ]
-        for j in range(CH):
-            wait_bytes(rsrecv.at[j, pl.ds(0, PEERS - 1)], rs_r.at[j])
-            total = rsrecv[j, 0].astype(F32)
-            for p in range(1, PEERS):
-                total = total + rsrecv[j, p].astype(F32)
-            xsend[j] = total.astype(BF16)
-            xcopy[j].start()
-
         gain = jnp.where(t == 0, 1.0, 2.0).astype(F32)
         back = jnp.where(t == 0, 0.0, 1.0).astype(F32)
         for j in range(CH):
-            xcopy[j].wait_recv()
-            image = xsend[j].astype(F32) + xrecv[par, j].astype(F32)
+            wait_bytes(rsrecv.at[j, pl.ds(0, PEERS - 1)], rs_r.at[j])
+            image = rsrecv[j, 0].astype(F32)
+            for p in range(1, PEERS):
+                image = image + rsrecv[j, p].astype(F32)
             now = cur[j]
             mapped = (2.0 / spread) * image - now
             following = gain * mapped - back * prev[j]
@@ -271,31 +271,29 @@
             @pl.when(t < ITERS - 1)
             def _(j=j, following=following):
                 vg[j, me] = following.astype(BF16)
-                for dy, dz in OFFSETS:
+                for off in OFFSETS:
                     rcopy(
-                        vg.at[j, me], vg.at[j, me], ag_s.at[j], ag_r.at[j], peer(dy, dz)
+                        vg.at[j, me], vg.at[j, me], ag_s.at[j], ag_r.at[j], peer(*off)
                     ).start()
 
         mom[pl.ds(t + 1, 1), :] = dots()
         for j in range(CH):
-            xcopy[j].wait_send()
             wait_bytes(rssend.at[j, pl.ds(0, PEERS - 1)], rs_s.at[j])
         return carry
 
     lax.fori_loop(0, ITERS, step, 0)
 
     momrecv[me] = mom[...]
-    for dy, dz in OFFSETS:
-        rcopy(mom, momrecv.at[me], m_s, m_r, peer(dy, dz)).start()
-    for q in range(8):
-        for j in range(CH):
-            four = cur[j, 4 * q:4 * q + 4, :]
-            finsend[q, 2 * j:2 * j + 2, :] = jnp.where(h == 0, four[0:2], four[2:4])
-    for dy, dz in OFFSETS:
+    for off in OFFSETS:
+        rcopy(mom, momrecv.at[me], m_s, m_r, peer(*off)).start()
+    for q in range(PR // 2):
+        for j in range(CH):
+            finsend[q, 2 * j:2 * j + 2, :] = cur[j, 2 * q:2 * q + 2, :]
+    for off in OFFSETS:
         rcopy(
-            finsend.at[lax.rem(peer_index(dy, dz), 8)], finrecv.at[me], f_s, f_r, peer(dy, dz)
+            finsend.at[lax.rem(peer_index(*off), PR // 2)], finrecv.at[me], f_s, f_r, peer(*off)
         ).start()
-    finrecv[me] = finsend[lax.rem(me, 8)]
+    finrecv[me] = finsend[lax.rem(me, PR // 2)]
 
     wait_bytes(momrecv.at[pl.ds(0, PEERS - 1)], m_r)
     total = momrecv[0]
@@ -306,11 +304,11 @@
     for who in (core_id, lo_id, diag_id):
         rcopy(momx.at[slot], momx.at[slot], q_s, q_r, who).start()
     wait_bytes(finrecv.at[pl.ds(0, PEERS - 1)], f_r)
-    half = me // 8
+    part = me // (PR // 2)
     for k in range(TILES):
         for j in range(CH):
             col = (j * TILES + k) * LANES
-            out_ref[:, col:col + LANES] = finrecv[2 * k + half, 2 * j:2 * j + 2, :]
+            out_ref[:, col:col + LANES] = finrecv[PARTS * k + part, 2 * j:2 * j + 2, :]
     wait_bytes(momx.at[pl.ds(0, 3)], q_r)
     moments = jnp.sum(
         (momx[0] + momx[1]) + (momx[2] + momx[3]), axis=1, keepdims=True
@@ -359,12 +357,10 @@
             vm((2 * NCH, NP, RH), BF16),
             vm((CH, PEERS, PR, LANES), BF16),
             vm((CH, PEERS, PR, LANES), BF16),
-            vm((CH, PR, LANES), BF16),
-            vm((2, CH, PR, LANES), BF16),
             vm((CH, PR, LANES), F32),
             vm((CH, PR, LANES), F32),
             vm((CH, PR, LANES), F32),
-            vm((8, 2 * CH, LANES), F32),
+            vm((PR // 2, 2 * CH, LANES), F32),
             vm((PEERS, 2 * CH, LANES), F32),
             vm((16, LANES), F32),
             vm((PEERS, 16, LANES), F32),
@@ -374,7 +370,6 @@
             dma((NCH,)), dma((2, NCH)),
             dma((NCH,)), dma((NCH,)),
             dma((CH,)), dma((CH,)),
-            dma((CH,)), dma((2, CH)),
             dma((CH,)), dma((CH,)),
             dma, dma, dma, dma, dma, dma,
         ],

time: 235 us -> 237 us (level)
  no operation moved by 1% of the time
where the time goes in v3:
time: 237 us
  Pallas kernels  232 us (98%)
  local copies, waits for them, and re-layouts  2.55 us (1%)
  between operations  2.38 us (1%)
    pallas_call x1, Pallas kernels, per_device(): pl.pallas_call(kernel, out_shape=(jax.ShapeDtypeStruct((2, COLS), F32), j...  232 us

profile of v3, /device:TPU:1, one launch (start us, length us, event | category | flops | bytes accessed | tf_op | source)
XLA Modules:
  0.0 236.6 jit_solution(8461610937996800641)
XLA Ops:
  0.6 231.6 %cheb.1 = (f32[2,4096]{1,0:T(2,128)}, f32[9]{0:T(128)}, f32[1]{0:T(128)}) custom-call(bf16[2048,4096]{1,0:T(8,128)(2,1)} %b_hbm.1, f32[8,1,256]{2,1,0:T(1,128)} %bitcast.5, f32[64,4096]{1,0:T(8,128)} %bitcast.3), custom_call_target="tpu_custom_call" | custom-call | tf_op jit(solution)/shard_map/cheb/pallas_call | solution.py:329
  232.3 1.4 copy.9
  233.6 1.2 copy.10

commit v4 on v3

--- a/solution.py
+++ b/solution.py
@@ -19,7 +19,7 @@
 ROWS = 2048
 COLS = 4096
 NP = 64
-CH = 2
+CH = 4
 WIDE = COLS // CH
 TILES = WIDE // 128
 OWNERS = 32
@@ -110,7 +110,7 @@
             ].T
             return carry
 
-        lax.fori_loop(0, COLS // 256, flip, 0)
+        lax.fori_loop(0, COLS // 256, flip, 0, unroll=4)
 
     flip_rows(0)
     zload.wait()

time: 237 us -> 214 us (0.903)
  Pallas kernels: 232 us -> 209 us
    pallas_call x1, Pallas kernels: 232 us -> 209 us  [per_device(): pl.pallas_call(kernel, out_shape=(jax.ShapeDtypeStruct((2, COLS), F32), j...]
where the time goes in v4:
time: 214 us
  Pallas kernels  209 us (98%)
  local copies, waits for them, and re-layouts  2.55 us (1%)
  between operations  2.38 us (1%)
    pallas_call x1, Pallas kernels, per_device(): pl.pallas_call(kernel, out_shape=(jax.ShapeDtypeStruct((2, COLS), F32), j...  209 us

profile of v4, /device:TPU:1, one launch (start us, length us, event | category | flops | bytes accessed | tf_op | source)
XLA Modules:
  0.0 214.2 jit_solution(7049344847239883970)
XLA Ops:
  0.6 209.3 %cheb.1 = (f32[2,4096]{1,0:T(2,128)}, f32[9]{0:T(128)}, f32[1]{0:T(128)}) custom-call(bf16[2048,4096]{1,0:T(8,128)(2,1)} %b_hbm.1, f32[8,1,256]{2,1,0:T(1,128)} %bitcast.5, f32[64,4096]{1,0:T(8,128)} %bitcast.3), custom_call_target="tpu_custom_call" | custom-call | tf_op jit(solution)/shard_map/cheb/pallas_call | solution.py:329
  210.0 1.4 copy.9
  211.3 1.2 copy.10

commit v5 on v4

--- a/solution.py
+++ b/solution.py
@@ -51,6 +51,12 @@
     return np.array(values)
 
 
+def padded_dot(a, b):
+    rows = a.shape[0]
+    full = jnp.concatenate([a, jnp.zeros((128 - rows, a.shape[1]), a.dtype)], axis=0)
+    return jnp.dot(full, b, preferred_element_type=F32)[:rows]
+
+
 def kernel(
     b_hbm, w_ref, z_hbm, out_ref, mom_out, energy_out,
     bmat, bt, zbuf, vg, racc, own_half, asend, arecv, bsend, brecv, sbuf,
@@ -63,6 +69,7 @@
     xl = lax.axis_index("aux_0")
     core = lax.axis_index("aux_1")
     me = (y * 4 + z) * 2 + h
+    slot = xl * 2 + core
 
     def peer(dy, dz, dh):
         return {
@@ -127,19 +134,14 @@
         cur[j] = blk
         prev[j] = blk
 
-    def dots():
-        acc = prob[0] * cur[0]
+    def dots(left):
+        acc = left[0] * cur[0]
         for j in range(1, CH):
-            acc = acc + prob[j] * cur[j]
+            acc = acc + left[j] * cur[j]
         return jnp.sum(acc, axis=0, keepdims=True)
 
     mom[...] = jnp.zeros_like(mom)
-    mom[0:1, :] = dots()
-    for r in range(1, ROWS // 256):
-        flip_rows(r)
-
-    pl.semaphore_wait(barrier, len(everyone))
-
+    mom[0:1, :] = dots(prob)
     def vector(j):
         return jnp.concatenate(
             [
@@ -149,26 +151,33 @@
             axis=1,
         )
 
+    def rows_part(j, i):
+        return padded_dot(
+            vector(j), bt[j * WIDE:(j + 1) * WIDE, i * RCH:(i + 1) * RCH]
+        )
+
+    for r in range(1, ROWS // 256):
+        flip_rows(r)
+        if r % 2 == 1:
+            i = r // 2
+            part = rows_part(0, i)
+            for j in range(1, CH - 1):
+                part = part + rows_part(j, i)
+            racc[i] = part
+
+    pl.semaphore_wait(barrier, len(everyone))
+
     def step(t, carry):
         par = lax.rem(t, 2)
-
-        def rows_part(j, i):
-            return jnp.dot(
-                vector(j),
-                bt[j * WIDE:(j + 1) * WIDE, i * RCH:(i + 1) * RCH],
-                preferred_element_type=F32,
-            )
 
         for j in range(CH):
             @pl.when(t > 0)
             def _(j=j):
                 wait_bytes(vg.at[j, pl.ds(0, PEERS - 1)], ag_r.at[j])
-
-            if j == CH - 1:
-                break
-            for i in range(NCH):
-                part = rows_part(j, i)
-                racc[i] = part if j == 0 else racc[i] + part
+                if j < CH - 1:
+                    for i in range(NCH):
+                        part = rows_part(j, i)
+                        racc[i] = part if j == 0 else racc[i] + part
 
         acopy = [
             rcopy(asend.at[i], arecv.at[i], a_s.at[i], a_r.at[i], core_id) for i in range(NCH)
@@ -231,9 +240,7 @@
                     ys = [2 * side + low, 2 * side + 1 - low]
                     ys = ys if k == 0 else ys[::-1]
                 col = pl.multiple_of(j * WIDE + side * 512, 512)
-                img = jnp.dot(
-                    scaled(), bmat[:, pl.ds(col, 512)], preferred_element_type=F32
-                ).astype(BF16)
+                img = padded_dot(scaled(), bmat[:, pl.ds(col, 512)]).astype(BF16)
                 for q in range(4):
                     for g in range(PARTS):
                         rssend[j, (side * 4 + q) * PARTS + g] = img[
@@ -250,6 +257,16 @@
                         ).start()
             rsrecv[j, me] = rssend[j, me]
 
+        @pl.when(t == ITERS - 1)
+        def _():
+            wait_bytes(momrecv.at[pl.ds(0, PEERS - 1)], m_r)
+            total = momrecv[0]
+            for p in range(1, PEERS):
+                total = total + momrecv[p]
+            momx[slot] = total
+            for who in (core_id, lo_id, diag_id):
+                rcopy(momx.at[slot], momx.at[slot], q_s, q_r, who).start()
+
         for i in range(NCH):
             acopy[i].wait_send()
             bcopy[i].wait_send()
@@ -276,16 +293,26 @@
                         vg.at[j, me], vg.at[j, me], ag_s.at[j], ag_r.at[j], peer(*off)
                     ).start()
 
-        mom[pl.ds(t + 1, 1), :] = dots()
+        @pl.when(t < ITERS - 1)
+        def _():
+            mom[pl.ds(t + 1, 1), :] = dots(prob)
+
+        @pl.when(t == ITERS // 2 - 1)
+        def _():
+            mom[ITERS:ITERS + 1, :] = dots(cur)
+
+        @pl.when(t == ITERS - 2)
+        def _():
+            momrecv[me] = mom[...]
+            for off in OFFSETS:
+                rcopy(mom, momrecv.at[me], m_s, m_r, peer(*off)).start()
+
         for j in range(CH):
             wait_bytes(rssend.at[j, pl.ds(0, PEERS - 1)], rs_s.at[j])
         return carry
 
     lax.fori_loop(0, ITERS, step, 0)
 
-    momrecv[me] = mom[...]
-    for off in OFFSETS:
-        rcopy(mom, momrecv.at[me], m_s, m_r, peer(*off)).start()
     for q in range(PR // 2):
         for j in range(CH):
             finsend[q, 2 * j:2 * j + 2, :] = cur[j, 2 * q:2 * q + 2, :]
@@ -295,29 +322,22 @@
         ).start()
     finrecv[me] = finsend[lax.rem(me, PR // 2)]
 
-    wait_bytes(momrecv.at[pl.ds(0, PEERS - 1)], m_r)
-    total = momrecv[0]
-    for p in range(1, PEERS):
-        total = total + momrecv[p]
-    slot = xl * 2 + core
-    momx[slot] = total
-    for who in (core_id, lo_id, diag_id):
-        rcopy(momx.at[slot], momx.at[slot], q_s, q_r, who).start()
-    wait_bytes(finrecv.at[pl.ds(0, PEERS - 1)], f_r)
-    part = me // (PR // 2)
-    for k in range(TILES):
-        for j in range(CH):
-            col = (j * TILES + k) * LANES
-            out_ref[:, col:col + LANES] = finrecv[PARTS * k + part, 2 * j:2 * j + 2, :]
     wait_bytes(momx.at[pl.ds(0, 3)], q_r)
     moments = jnp.sum(
         (momx[0] + momx[1]) + (momx[2] + momx[3]), axis=1, keepdims=True
     ) * (1.0 / (NP * COLS * 4))
     energy = jnp.zeros((), F32)
     for k, c in enumerate(cheb_coefficients(ITERS + 1)):
-        mom_out[k] = moments[k, 0]
-        energy = energy + moments[k, 0] * float(c)
+        value = moments[k, 0] if k < ITERS else 2.0 * moments[k, 0] - moments[0, 0]
+        mom_out[k] = value
+        energy = energy + value * float(c)
     energy_out[0] = energy
+    wait_bytes(finrecv.at[pl.ds(0, PEERS - 1)], f_r)
+    part = me // (PR // 2)
+    for k in range(TILES):
+        for j in range(CH):
+            col = (j * TILES + k) * LANES
+            out_ref[:, col:col + LANES] = finrecv[PARTS * k + part, 2 * j:2 * j + 2, :]
     wait_bytes(momrecv.at[pl.ds(0, PEERS - 1)], m_s)
     wait_bytes(finrecv.at[pl.ds(0, PEERS - 1)], f_s)
     wait_bytes(momx.at[pl.ds(0, 3)], q_s)

time: 214 us -> 210 us (0.981)
  Pallas kernels: 209 us -> 205 us
    pallas_call x1, Pallas kernels: 209 us -> 205 us  [per_device(): pl.pallas_call(kernel, out_shape=(jax.ShapeDtypeStruct((2, COLS), F32), j...]
where the time goes in v5:
time: 210 us; the launch traced here: 209 us
  Pallas kernels  205 us (98%)
  local copies, waits for them, and re-layouts  2.55 us (1%)
  between operations  2.38 us (1%)
    pallas_call x1, Pallas kernels, per_device(): pl.pallas_call(kernel, out_shape=(jax.ShapeDtypeStruct((2, COLS), F32), j...  205 us

profile of v5, /device:TPU:1, one launch (start us, length us, event | category | flops | bytes accessed | tf_op | source)
XLA Modules:
  0.0 209.5 jit_solution(5393098683942204944)
XLA Ops:
  0.6 204.5 %cheb.1 = (f32[2,4096]{1,0:T(2,128)}, f32[9]{0:T(128)}, f32[1]{0:T(128)}) custom-call(bf16[2048,4096]{1,0:T(8,128)(2,1)} %b_hbm.1, f32[8,1,256]{2,1,0:T(1,128)} %bitcast.5, f32[64,4096]{1,0:T(8,128)} %bitcast.3), custom_call_target="tpu_custom_call" | custom-call | tf_op jit(solution)/shard_map/cheb/pallas_call | solution.py:349
  205.2 1.4 copy.9
  206.5 1.2 copy.10

commit v6 on v5

--- a/solution.py
+++ b/solution.py
@@ -59,7 +59,7 @@
 
 def kernel(
     b_hbm, w_ref, z_hbm, out_ref, mom_out, energy_out,
-    bmat, bt, zbuf, vg, racc, own_half, asend, arecv, bsend, brecv, sbuf,
+    bmat, bt, zbuf, vg, racc, iacc, own_half, asend, arecv, bsend, brecv, sbuf,
     rssend, rsrecv, prob, prev, cur, finsend, finrecv, mom, momrecv, momx,
     load_sem, a_s, a_r, b_s, b_r, c_s, c_r, rs_s, rs_r, ag_s, ag_r, f_s, f_r, m_s, m_r, q_s, q_r,
 ):
@@ -223,11 +223,16 @@
 
         for i in range(NCH):
             third(i)
+        def half_image(who, col):
+            pieces = [bmat[pl.ds(pl.multiple_of((2 * i + who) * RH, RH), RH), pl.ds(col, 512)] for i in range(NCH)]
+            left = jnp.concatenate([sbuf[2 * i + who] for i in range(NCH)], axis=1)
+            return padded_dot(left, jnp.concatenate(pieces, axis=0))
+
+        for n in range(COLS // 512):
+            iacc[n] = half_image(core, n * 512)
+
         for i in range(NCH):
             ccopy[i].wait_recv()
-
-        def scaled():
-            return jnp.concatenate([sbuf[q] for q in range(2 * NCH)], axis=1)
 
         for j in range(CH):
             for k in range(TILES // 4):
@@ -240,7 +245,7 @@
                     ys = [2 * side + low, 2 * side + 1 - low]
                     ys = ys if k == 0 else ys[::-1]
                 col = pl.multiple_of(j * WIDE + side * 512, 512)
-                img = padded_dot(scaled(), bmat[:, pl.ds(col, 512)]).astype(BF16)
+                img = (iacc[j * (WIDE // 512) + side] + half_image(1 - core, col)).astype(BF16)
                 for q in range(4):
                     for g in range(PARTS):
                         rssend[j, (side * 4 + q) * PARTS + g] = img[
@@ -369,6 +374,7 @@
             vm((NP, COLS), F32),
             vm((CH, PEERS, PR, LANES), BF16),
             vm((NCH, NP, RCH), F32),
+            vm((COLS // 512, NP, 512), F32),
             vm((NCH, NP, RH), F32),
             vm((NCH, NP, RH), BF16),
             vm((NCH, NP, RH), BF16),

time: 210 us -> 214 us (1.019)
  Pallas kernels: 205 us -> 208 us
    pallas_call x1, Pallas kernels: 205 us -> 208 us  [per_device(): pl.pallas_call(kernel, out_shape=(jax.ShapeDtypeStruct((2, COLS), F32), j...]
where the time goes in v6:
time: 214 us; the launch traced here: 213 us
  Pallas kernels  208 us (97%)
  local copies, waits for them, and re-layouts  2.55 us (1%)
  between operations  2.38 us (1%)
    pallas_call x1, Pallas kernels, per_device(): pl.pallas_call(kernel, out_shape=(jax.ShapeDtypeStruct((2, COLS), F32), j...  208 us

profile of v6, /device:TPU:1, one launch (start us, length us, event | category | flops | bytes accessed | tf_op | source)
XLA Modules:
  0.0 213.3 jit_solution(11683962186024624769)
XLA Ops:
  0.6 208.4 %cheb.1 = (f32[2,4096]{1,0:T(2,128)}, f32[9]{0:T(128)}, f32[1]{0:T(128)}) custom-call(bf16[2048,4096]{1,0:T(8,128)(2,1)} %b_hbm.1, f32[8,1,256]{2,1,0:T(1,128)} %bitcast.5, f32[64,4096]{1,0:T(8,128)} %bitcast.3), custom_call_target="tpu_custom_call" | custom-call | tf_op jit(solution)/shard_map/cheb/pallas_call | solution.py:354
  209.0 1.4 copy.9
  210.4 1.2 copy.10
